TPU v7x, 32 devices: a whole 2x2x4 slice. The times are simulated.
32 devices in a mesh: facet: 8 (over y, x, core), sub: 4 (over z).
Axes of the slice: x: 2, y: 2, z: 4, core: 2. Of those that a mesh axis runs over, the one named last changes fastest.
Arguments:
- model_image: float32 [8, 128, 8192], P('facet'), may hold values from -6 to 6
- step_sizes: float32 [2], replicated, may hold values from 0.3 to 1
- facet_offsets: int32 [2, 8], replicated, may hold values from 0 to 57344
- col_offsets: int32 [4], P('sub'), may hold values from 0 to 65280
- row_offsets: int32 [4, 8], P('sub'), may hold values from 0 to 65280
- counts: int32 [4, 8], P('sub'), may hold values from 1024 to 4096, as said below
- vis_uv: int32 [2, 4, 8, 4096], P(None, 'sub', 'facet'), may hold values from 32 to 2015
- vis_obs: bfloat16 [2, 4, 8, 4096], P(None, 'sub', 'facet'), may hold values from -6 to 6
- vis_weight: bfloat16 [4, 8, 4096], P('sub', 'facet'), may hold values from 0.25 to 4
Outputs:
- updated_image: float32 [8, 128, 8192], P('facet')
- residual_vis: float32 [2, 4, 8, 4096], P(None, 'sub', 'facet')
Inputs may be any that keep to these rules, and one draw needn't show every extreme that they name: The visibilities of a subgrid fill its first counts slots; every draw has a subgrid with exactly 4096 visibilities and one with exactly 1024.
All inputs are finite; a program needn't handle non-finite values.
Results may differ from a plain program's by a relative error of at most 0.017.
Values may be sent and summed in bfloat16 or wider, within the bound.
A program may use at most 64 MiB of HBM per device.

v0:
```python
import math

import jax
import jax.numpy as jnp
from jax import lax
from jax.sharding import PartitionSpec as P

NIMG = 65536
FW = 8192
FROWS = 128
SGW = 256
VCAP = 4096
VB = 512
OS = 8
KSUP = 4
ITERS = 2


two_pi = 2.0 * math.pi


def phase_index(frequency, pixels):
    pixel_low = pixels % 256
    pixel_high = pixels // 256
    return (frequency * pixel_low + frequency * pixel_high % (NIMG // 256) * 256) % NIMG


def row_table(frequency_start, pixel_start):
    frequency = frequency_start + jnp.arange(SGW, dtype=jnp.int32)
    pixels = pixel_start + jnp.arange(FROWS, dtype=jnp.int32)
    angles = phase_index(frequency[:, None], pixels[None, :]).astype(jnp.float32) * (two_pi / NIMG)
    return jnp.concatenate([jnp.cos(angles), jnp.sin(angles)], axis=1).astype(jnp.bfloat16)


def column_table(frequency_start, pixel_start):
    frequency = frequency_start + jnp.arange(SGW, dtype=jnp.int32)
    pixels = pixel_start + jnp.arange(FW, dtype=jnp.int32)
    angles = phase_index(frequency[None, :], pixels[:, None]).astype(jnp.float32) * (two_pi / NIMG)
    return jnp.concatenate([jnp.cos(angles), -jnp.sin(angles)], axis=1).astype(jnp.bfloat16)


def expand_section(section_rows):
    real_half = section_rows[:, :SGW]
    imag_half = section_rows[:, SGW:]
    lower_rows = jnp.concatenate([imag_half, -real_half], axis=1)
    return jnp.concatenate([section_rows, lower_rows], axis=0)


def fold_back(back_rows):
    real_part = back_rows[..., :FROWS, :SGW] - back_rows[..., FROWS:, SGW:]
    imag_part = back_rows[..., :FROWS, SGW:] + back_rows[..., FROWS:, :SGW]
    return jnp.concatenate([real_part, imag_part], axis=-1)


def kernel_rows(position):
    offset = (jnp.arange(SGW, dtype=jnp.int32) * OS + OS // 2)[None, :] - position[:, None]
    distance = offset.astype(jnp.float32) / OS
    inside = jnp.abs(offset) <= KSUP * OS
    return jnp.where(inside, jnp.exp(-0.5 * distance * distance), 0.0).astype(jnp.bfloat16)


def block_pass(grid_bf, row_positions, column_positions, observed, weight, is_live):
    row_kernel = kernel_rows(row_positions)
    column_kernel = kernel_rows(column_positions)
    sampled = jnp.dot(row_kernel, grid_bf, preferred_element_type=jnp.float32)
    column_float = column_kernel.astype(jnp.float32)
    predicted_real = jnp.sum(sampled[:, :SGW] * column_float, axis=1)
    predicted_imag = jnp.sum(sampled[:, SGW:] * column_float, axis=1)
    weight_float = weight.astype(jnp.float32)
    residual_real = jnp.where(
        is_live, weight_float * (observed[0].astype(jnp.float32) - predicted_real), 0.0
    )
    residual_imag = jnp.where(
        is_live, weight_float * (observed[1].astype(jnp.float32) - predicted_imag), 0.0
    )
    weighted = jnp.concatenate(
        [residual_real[:, None] * column_float, residual_imag[:, None] * column_float], axis=1
    ).astype(jnp.bfloat16)
    block_grid = lax.dot_general(
        row_kernel, weighted, (((0,), (0,)), ((), ())), preferred_element_type=jnp.float32
    )
    return (block_grid, jnp.stack([residual_real, residual_imag]))


def sweep_blocks(grid_bf, positions, observed, weight, live_total, blocks):
    length = positions.shape[1]

    def one_block(block_index, running):
        grid_sum, residual = running
        first_row = (block_index * VB).astype(jnp.int32)
        position_part = lax.dynamic_slice_in_dim(positions, first_row, VB, 1)
        observed_part = lax.dynamic_slice_in_dim(observed, first_row, VB, 1)
        weight_part = lax.dynamic_slice_in_dim(weight, first_row, VB, 0)
        is_live = first_row + jnp.arange(VB, dtype=jnp.int32) < live_total
        block_grid, values = block_pass(
            grid_bf, position_part[0], position_part[1], observed_part, weight_part, is_live
        )
        residual = lax.dynamic_update_slice(residual, values, (jnp.int32(0), first_row))
        return (grid_sum + block_grid, residual)

    starting = (jnp.zeros((SGW, 2 * SGW), jnp.float32), jnp.zeros((2, length), jnp.float32))
    return lax.fori_loop(0, blocks, one_block, starting)


def local(
    model_image,
    step_sizes,
    facet_offsets,
    col_offsets,
    row_offsets,
    counts,
    vis_uv,
    vis_obs,
    vis_weight,
):
    facet_count = lax.axis_size("facet")
    norm_factor = 1.0 / math.sqrt(facet_count * FROWS * FW)
    my_facet = lax.axis_index("facet")
    columns_factor = column_table(col_offsets[0], facet_offsets[1, my_facet])
    my_rows = row_offsets[0]
    column_rows = jax.vmap(lambda single: row_table(single, facet_offsets[0, my_facet]))(my_rows)
    facet_rows = jax.vmap(lambda offset: row_table(my_rows[my_facet], offset))(facet_offsets[0])
    own_count = counts[0, my_facet]
    positions = vis_uv[:, 0, 0]
    observed = vis_obs[:, 0, 0]
    weight = vis_weight[0, 0]
    model_now = model_image[0]
    residual = jnp.zeros((2, VCAP), jnp.float32)
    for cycle_index in range(ITERS):
        section_rows = jnp.dot(
            model_now.astype(jnp.bfloat16), columns_factor, preferred_element_type=jnp.float32
        ).astype(jnp.bfloat16)
        pieces = lax.all_gather(section_rows[None], "facet", axis=0, tiled=True)
        expanded_pieces = jax.vmap(expand_section)(pieces)
        summed = lax.dot_general(
            facet_rows,
            expanded_pieces,
            (((0, 2), (0, 1)), ((), ())),
            preferred_element_type=jnp.float32,
        )
        grid_bf = (norm_factor * summed).astype(jnp.bfloat16)
        gridded, residual = sweep_blocks(
            grid_bf, positions, observed, weight, own_count, (own_count + VB - 1) // VB
        )
        gridded_bf = gridded.astype(jnp.bfloat16)
        add_pieces = lax.all_gather(gridded_bf[None], "facet", axis=0, tiled=True)
        add_number = add_pieces.shape[0]
        back_rows = lax.dot_general(
            column_rows.reshape(add_number * SGW, 2 * FROWS),
            add_pieces.reshape(add_number * SGW, 2 * SGW),
            (((0,), (0,)), ((), ())),
            preferred_element_type=jnp.float32,
        )
        adjoint_rows = fold_back(back_rows).astype(jnp.bfloat16)
        partial_gradient = lax.dot_general(
            adjoint_rows,
            columns_factor,
            (((1,), (1,)), ((), ())),
            preferred_element_type=jnp.float32,
        )
        gradient = lax.psum(partial_gradient.astype(jnp.bfloat16), "sub").astype(jnp.float32)
        model_now = model_now + step_sizes[cycle_index] * (norm_factor * gradient)
    return (model_now[None], residual.reshape(2, 1, 1, VCAP))


def solution(mesh):
    in_specs = (
        P("facet", None, None),
        P(),
        P(),
        P("sub"),
        P("sub", None),
        P("sub", None),
        P(None, "sub", "facet", None),
        P(None, "sub", "facet", None),
        P("sub", "facet", None),
    )
    out_specs = (P("facet", None, None), P(None, "sub", "facet", None))
    return jax.shard_map(local, mesh=mesh, in_specs=in_specs, out_specs=out_specs, check_vma=False)
```

profile of v0, /device:TPU:0, one launch (start us, length us, event | category | flops | bytes accessed | tf_op | source)
XLA Modules:
  0.0 419.5 jit_solution(10102998328427896458)
XLA Ops:
  7.2 1.4 constant_dynamic-slice_fusion.4
  8.7 0.7 add_select_fusion.6
  10.0 42.6 %cosine_convert_fusion = (bf16[8192,256]{1,0:T(8,128)(2,1)S(1)}, bf16[8192,256]{1,0:T(8,128)(2,1)S(1)}) fusion(s32[8192]{0:T(1024)S(1)} %get-tuple-element.372, s32[8192]{0:T(1024)S(1)} %get-tuple-element.373, s32[256]{0:T(256)S(1)} %iota_add_fusion.3), kind=kLoop, calls=%fused_computation.117 | loop fusion | flops 65011712 | bytes 8455168 | tf_op jit(solution)/shard_map/convert.12
  52.6 1.9 copy-done.2
  54.5 1.4 copy-done.5
  56.0 3.1 fusion.115
  59.1 0.6 constant_dynamic-slice_fusion.3
  60.4 0.6 constant_dynamic-slice_fusion.2
  61.1 0.6 iota_add_fusion.4
  61.9 5.0 %cosine_convert_fusion.1 = (bf16[8,256,128]{2,1,0:T(8,128)(2,1)S(1)}, bf16[8,256,128]{2,1,0:T(8,128)(2,1)S(1)}) fusion(s32[8,128]{1,0:T(8,128)S(1)} %get-tuple-element.369, s32[8,128]{1,0:T(8,128)S(1)} %get-tuple-element.368, s32[256]{0:T(256)S(1)} %iota_add_fusion.4), kind=kLoop, calls=%fused_computation.179 | loop fusion | flops 7864320 | bytes 1057792 | tf_op jit(solution)/shard_map/convert.14
  66.8 18.6 %all-gather.9.cloned.1.call-done = bf16[1024,512]{0,1:T(8,128)(2,1)} async-done(((bf16[128,512]{0,1:T(8,128)(2,1)}), bf16[1024,512]{0,1:T(8,128)(2,1)}) %all-gather.9.cloned.1.call-update) | async-done | bytes 1048592 | tf_op jit(solution)/shard_map/all_gather | solution.py:133
  85.4 1.5 copy.18
  87.0 0.7 fusion.108
  87.8 5.2 %while.30 = (s32[]{:T(128)}, f32[256,512]{1,0:T(8,128)S(1)}, s32[]{:T(128)}, s32[2,4096]{1,0:T(2,128)S(1)}, s32[]{:T(128)}, /*index=5*/bf16[4096]{0:T(1024)(128)...) while((s32[]{:T(128)}, f32[256,512]{1,0:T(8,128)S(1)}, ...), condition=%wide.region_3.4_spmd, body=%wide.region_0.3_spmd.sunk | while | flops 275649536 | bytes 4505811 | solution.py:102
  87.9 0.5 fusion.191
  88.5 0.4 fusion.192
  88.9 0.7 fusion.193
  89.9 0.4 convolution_add_fusion.4
  90.5 0.5 fusion.191
  91.0 0.4 fusion.192
  91.5 0.7 fusion.193
  92.5 0.4 convolution_add_fusion.4
  93.0 0.7 convert_element_type.203
  94.0 0.7 and_select_fusion
  94.8 5.0 %cosine_convert_fusion.2 = (bf16[8,256,128]{2,1,0:T(8,128)(2,1)S(1)}, bf16[8,256,128]{2,1,0:T(8,128)(2,1)S(1)}) fusion(s32[128]{0:T(128)S(1)} %get-tuple-element.370, s32[128]{0:T(128)S(1)} %get-tuple-element.371, s32[8,256]{1,0:T(8,128)S(1)} %iota_add_fusion.1), kind=kLoop, calls=%fused_computation.181 | loop fusion | flops 7864320 | bytes 1057792 | tf_op jit(solution)/shard_map/convert.16
  99.8 35.3 %all-gather.11.cloned.1.call-done = bf16[2048,512]{1,0:T(8,128)(2,1)} async-done(((bf16[256,512]{1,0:T(8,128)(2,1)}), bf16[2048,512]{1,0:T(8,128)(2,1)}) %all-gather.11.cloned.1.call-update) | async-done | bytes 2097168 | tf_op jit(solution)/shard_map/all_gather | solution.py:146
  135.1 2.5 convolution_bitcast_fusion.1
  137.9 6.4 %convolution_convert_fusion.1 = bf16[128,8192]{1,0:T(8,128)(2,1)} fusion(bf16[128,256]{1,0:T(8,128)(2,1)S(1)} %get-tuple-element.357, bf16[128,256]{1,0:T(8,128)(2,1)S(1)} %get-tuple-element.356, bf16[8192,256]{1,0:T(8,128)(2,1)} %copy-done.5, bf16[8192,256]{1,0:T(8,128)(2,1)S(1)} %copy-done.3), kind=kOutput, calls=%fused_computation.108 | convolution fusion | flops 1091829760 | bytes 10616832 | tf_op jit(solution)/shard_map/dot_general | solution.py:155
  144.4 0.6 fusion.159
  145.6 85.0 %all-reduce.3.cloned.1.call-done = bf16[128,8192]{1,0:T(8,128)(2,1)} async-done(((bf16[128,8192]{1,0:T(8,128)(2,1)}), bf16[128,8192]{1,0:T(8,128)(2,1)}) %all-reduce.3.cloned.1.call-update) | async-done | bytes 2097168 | tf_op jit(solution)/shard_map/psum | solution.py:161
  230.6 7.1 %fusion.111 = bf16[128,512]{1,0:T(8,128)(2,1)} fusion(bf16[128,8192]{1,0:T(8,128)(2,1)} %all-reduce.3.cloned.1.call-done, f32[1,128,8192]{2,1,0:T(8,128)} %param.13, f32[]{:T(128)} %bitcast.23, bf16[8192,256]{1,0:T(8,128)(2,1)} %copy-done.5, bf16[8192,256]{1,0:T(8,128)(2,1)} %copy-done.2), kind=kOutput, calls=%fused_computation.161 | convolution fusion | flops 1094778880 | bytes 14811140 | tf_op jit(solution)/shard_map/dot_general | solution.py:130
  237.8 22.5 %all-gather.13.cloned.1.call-done = bf16[1024,512]{1,0:T(8,128)(2,1)} async-done(((bf16[128,512]{1,0:T(8,128)(2,1)}), bf16[1024,512]{1,0:T(8,128)(2,1)}) %all-gather.13.cloned.1.call-update) | async-done | bytes 1048592 | tf_op jit(solution)/shard_map/all_gather | solution.py:133
  260.4 1.3 fusion.157
  261.6 1.9 fusion.105
  263.7 5.2 %while.31 = (s32[]{:T(128)}, f32[256,512]{1,0:T(8,128)S(1)}, f32[2,4096]{1,0:T(2,128)S(1)}, s32[]{:T(128)}, s32[2,4096]{1,0:T(2,128)S(1)}, /*index=5*/s32[]{:T(1...) while((s32[]{:T(128)}, f32[256,512]{1,0:T(8,128)S(1)}, ...), condition=%wide.region_8.9_spmd, body=%wide.region_5.8_spmd.sunk | while | flops 275650560 | bytes 4514015 | solution.py:102
  263.8 0.5 fusion.200
  264.8 0.7 fusion.202
  265.8 0.4 convolution_add_fusion.5
  266.4 0.5 fusion.200
  267.4 0.7 fusion.202
  268.4 0.4 convolution_add_fusion.5
  268.9 0.7 convert_element_type.209
  269.7 41.5 %all-gather.15.cloned.1.call-done = bf16[2048,512]{1,0:T(8,128)(2,1)} async-done(((bf16[256,512]{1,0:T(8,128)(2,1)}), bf16[2048,512]{1,0:T(8,128)(2,1)}) %all-gather.15.cloned.1.call-update) | async-done | bytes 2097168 | tf_op jit(solution)/shard_map/all_gather | solution.py:146
  311.2 2.5 convolution_bitcast_fusion
  314.0 6.5 %convolution_convert_fusion = bf16[128,8192]{1,0:T(8,128)(2,1)} fusion(bf16[128,256]{1,0:T(8,128)(2,1)S(1)} %get-tuple-element.355, bf16[128,256]{1,0:T(8,128)(2,1)S(1)} %get-tuple-element.354, bf16[8192,256]{1,0:T(8,128)(2,1)} %copy-done.5, bf16[8192,256]{1,0:T(8,128)(2,1)S(1)} %copy-done.4), kind=kOutput, calls=%fused_computation.107 | convolution fusion | flops 1091829760 | bytes 10616832 | tf_op jit(solution)/shard_map/dot_general | solution.py:155
  321.1 0.6 reshape.276
  321.7 85.1 %all-reduce.5.cloned.1.call-done = bf16[128,8192]{1,0:T(8,128)(2,1)} async-done(((bf16[128,8192]{1,0:T(8,128)(2,1)}), bf16[128,8192]{1,0:T(8,128)(2,1)}) %all-reduce.5.cloned.1.call-update) | async-done | bytes 2097168 | tf_op jit(solution)/shard_map/psum | solution.py:161
  406.8 5.8 %add_bitcast_fusion = f32[1,128,8192]{2,1,0:T(8,128)} fusion(bf16[128,8192]{1,0:T(8,128)(2,1)} %all-reduce.5.cloned.1.call-done, bf16[128,8192]{1,0:T(8,128)(2,1)S(1)} %copy-done.6, f32[1,128,8192]{2,1,0:T(8,128)} %param.13, f32[]{:T(128)} %bitcast.28, f32[]{:T(128)} %bitcast.23), kind=kLoop, calls=%fused_computation.120 | loop fusion | flops 6291456 | bytes 12582920 | tf_op jit(solution)/shard_map/broadcast_in_dim | solution.py:163
  (68 shorter events, 4.4 us)
Async XLA Ops:
  7.2 52.0 %copy-start = (s32[1,8]{1,0:T(1,128)S(1)}, s32[1,8]{1,0:T(1,128)}, u32[]{:S(2)}) copy-start(s32[1,8]{1,0:T(1,128)} %param.18) | copy-start | bytes 100
  7.2 78.2 %all-gather.9.cloned.1.call-start = ((), (), s32[]{:S(2)}) async-start(), calls=%async_computation.2 | async-start | bytes 1179648 | tf_op jit(solution)/shard_map/all_gather | solution.py:133
  10.0 46.0 %copy-start.1 = (f32[1,128,8192]{2,1,0:T(8,128)S(1)}, f32[1,128,8192]{2,1,0:T(8,128)}, u32[]{:S(2)}) copy-start(f32[1,128,8192]{2,1,0:T(8,128)} %param.13) | copy-start | bytes 12582916
  52.6 2.0 copy-start.2
  52.6 3.4 copy-start.5
  56.0 4.4 %copy-start.12 = (s32[1,8]{1,0:T(1,128)S(1)}, s32[1,8]{1,0:T(1,128)}, u32[]{:S(2)}) copy-start(s32[1,8]{1,0:T(1,128)} %param.17) | copy-start | bytes 100
  56.0 5.0 %copy-start.8 = (s32[2,1,1,4096]{3,2,1,0:T(1,128)S(1)}, s32[2,1,1,4096]{3,2,1,0:T(1,128)}, u32[]{:S(2)}) copy-start(s32[2,1,1,4096]{3,2,1,0:T(1,128)} %param.19) | copy-start | bytes 98308
  56.0 5.1 %copy-start.9 = (bf16[1,1,4096]{2,1,0:T(2,128)(2,1)S(1)}, bf16[1,1,4096]{2,1,0:T(2,128)(2,1)}, u32[]{:S(2)}) copy-start(bf16[1,1,4096]{2,1,0:T(2,128)(2,1)} %param.21) | copy-start | bytes 24580
  56.0 5.8 %copy-start.11 = (s32[2,8]{1,0:T(2,128)S(1)}, s32[2,8]{1,0:T(2,128)}, u32[]{:S(2)}) copy-start(s32[2,8]{1,0:T(2,128)} %param.15) | copy-start | bytes 196
  59.1 76.0 %all-gather.11.cloned.1.call-start = ((), (), s32[]{:S(2)}) async-start(), calls=%async_computation.3 | async-start | bytes 2359296 | tf_op jit(solution)/shard_map/all_gather | solution.py:146
  87.0 0.8 copy-start.7
  93.8 136.9 %all-reduce.3.cloned.1.call-start = ((), (), s32[]{:S(2)}) async-start(), calls=%async_computation | async-start | bytes 4194304 | tf_op jit(solution)/shard_map/psum | solution.py:161
  135.1 2.8 copy-start.3
  137.9 6.5 %copy-start.10 = (f32[2]{0:T(128)S(1)}, f32[2]{0:T(128)}, u32[]{:S(2)}) copy-start(f32[2]{0:T(128)} %param.14) | copy-start | bytes 28
  144.3 116.0 %all-gather.13.cloned.1.call-start = ((), (), s32[]{:S(2)}) async-start(), calls=%async_computation.4 | async-start | bytes 1179648 | tf_op jit(solution)/shard_map/all_gather | solution.py:133
  237.8 73.4 %all-gather.15.cloned.1.call-start = ((), (), s32[]{:S(2)}) async-start(), calls=%async_computation.5 | async-start | bytes 2359296 | tf_op jit(solution)/shard_map/all_gather | solution.py:146
  269.6 137.2 %all-reduce.5.cloned.1.call-start = ((), (), s32[]{:S(2)}) async-start(), calls=%async_computation.1 | async-start | bytes 4194304 | tf_op jit(solution)/shard_map/psum | solution.py:161
  311.2 2.8 copy-start.4
  314.0 92.8 %copy-start.6 = (bf16[128,8192]{1,0:T(8,128)(2,1)S(1)}, bf16[128,8192]{1,0:T(8,128)(2,1)}, u32[]{:S(2)}) copy-start(bf16[128,8192]{1,0:T(8,128)(2,1)} %all-reduce.3.cloned.1.call-done) | copy-start | bytes 6291460
Sparse Core Ops, SparseCore 0:
  59.2 26.1 all-gather.8
  93.9 41.1 all-gather.10
  144.4 86.1 all-reduce.2
  237.9 22.3 all-gather.12
  269.8 41.3 all-gather.14
  320.6 86.1 all-reduce.4
where the time goes:
time: 422 us; the launch traced here: 419 us
  waiting for transfers between devices  288 us (68%)
  other arithmetic  69.4 us (16%)
  matrix products  34.6 us (8%)
  between operations  16.9 us (4%)
  local copies, waits for them, and re-layouts  9.85 us (2%)
    psum x2, waiting for transfers between devices, local(): lax.psum(partial_gradient.astype(jnp.bfloat16), 'sub').astype(jnp.float32)  170 us
    all_gather x2, waiting for transfers between devices, local(): add_pieces = lax.all_gather(gridded_bf[None], 'facet', axis=0, tiled=True)  76.8 us
    another operation x9, other arithmetic  53.9 us
    all_gather x2, waiting for transfers between devices, local(): pieces = lax.all_gather(section_rows[None], 'facet', axis=0, tiled=True)  41.1 us
    dot_general x2, matrix products, local(): lax.dot_general(adjoint_rows, columns_factor, (((1,), (1,)), ((), ())), p...  12.9 us
    dot_general x2, matrix products, local(): jnp.dot(model_now.astype(jnp.bfloat16), columns_factor, preferred_element...  10.2 us
  transfers between devices with their start and end apart: 6, of which 6 were waited for; matrix products, arithmetic and copies ran while one was open for 3% of the time, Pallas kernels for 0%

commit v1 on v0

v1 whole, which is shorter than its diff:
```python
import functools
import math

import jax
import jax.numpy as jnp
from jax import lax
from jax.experimental import pallas as pl
from jax.experimental.pallas import tpu as pltpu
from jax.sharding import PartitionSpec as P

NIMG = 65536
SGW = 256
VB = 512
OS = 8
KSUP = 4
ITERS = 2
STEP = 1024
CHUNKS = 4
MESH = pl.DeviceIdType.MESH
VMEM = pltpu.VMEM
F32 = jnp.float32
BF16 = jnp.bfloat16
two_pi = 2.0 * math.pi


def cis(frequency, pixels):
    index = (frequency * pixels) & (NIMG - 1)
    angles = index.astype(F32) * (two_pi / NIMG)
    return jnp.concatenate([jnp.cos(angles), jnp.sin(angles)], axis=-1)


def dirichlet(k, start, length):
    k = ((k + NIMG // 2) & (NIMG - 1)) - NIMG // 2
    half = math.pi / NIMG
    phase = ((k * (2 * start + length - 1)) & (2 * NIMG - 1)).astype(F32) * half
    top = jnp.sin(((k * length) & (2 * NIMG - 1)).astype(F32) * half)
    bottom = jnp.sin(k.astype(F32) * half)
    zero = k == 0
    ratio = jnp.where(zero, float(length), top / jnp.where(zero, 1.0, bottom))
    phase = jnp.where(zero, 0.0, phase)
    return ratio * jnp.cos(phase), ratio * jnp.sin(phase)


def section_kernel(norm, model_ref, b_ref, c_ref, tw_ref, s_ref, st_ref, table):
    step = pl.program_id(0)
    fine = c_ref.shape[0]

    @pl.when(step == 0)
    def _():
        cc, cs = c_ref[:, :SGW], c_ref[:, SGW:]
        for h in range(STEP // fine):
            bc, bs = b_ref[h : h + 1, :SGW], b_ref[h : h + 1, SGW:]
            rows = pl.ds(h * fine, fine)
            table[rows, :SGW] = (bc * cc - bs * cs).astype(BF16)
            table[rows, SGW:] = (-(bc * cs + bs * cc)).astype(BF16)
        s_ref[...] = jnp.zeros_like(s_ref)

    part = jnp.dot(model_ref[...].astype(BF16), table[...], preferred_element_type=F32)
    pr, pi = part[:, :SGW], part[:, SGW:]
    tc, ts = tw_ref[0, :, :SGW], tw_ref[0, :, SGW:]
    s_ref[:, :SGW] += pr * tc + pi * ts
    s_ref[:, SGW:] += pi * tc - pr * ts

    @pl.when(step == pl.num_programs(0) - 1)
    def _():
        st_ref[...] = s_ref[...].T.astype(BF16)


def section(model, b, c, tw, norm):
    rows, width = model.shape
    return pl.pallas_call(
        functools.partial(section_kernel, norm),
        grid=(width // STEP,),
        out_shape=(
            jax.ShapeDtypeStruct((rows, 2 * SGW), F32),
            jax.ShapeDtypeStruct((2 * SGW, rows), BF16),
        ),
        in_specs=[
            pl.BlockSpec((rows, STEP), lambda i: (0, i)),
            pl.BlockSpec(b.shape, lambda i: (0, 0)),
            pl.BlockSpec(c.shape, lambda i: (0, 0)),
            pl.BlockSpec((1, 1, 2 * SGW), lambda i: (i, 0, 0)),
        ],
        out_specs=(
            pl.BlockSpec((rows, 2 * SGW), lambda i: (0, 0)),
            pl.BlockSpec((2 * SGW, rows), lambda i: (0, 0)),
        ),
        scratch_shapes=[VMEM((STEP, 2 * SGW), BF16)],
        name="section",
    )(model, b, c, tw)


def peers(n, ns):
    me = lax.axis_index("facet")
    z = lax.axis_index("sub")
    core = lax.rem(me, 2)
    chip = me // 2
    partner = me + 1 - 2 * core
    others = [lax.rem(chip + d, n // 2) * 2 + core for d in range(1, n // 2)]
    sources = [lax.rem(chip - d + n // 2, n // 2) * 2 + core for d in range(1, n // 2)]
    columns = [lax.rem(z + d, ns) for d in range(1, ns)]
    return me, z, core, chip, partner, others, sources, columns


def greet(partner, others, columns):
    barrier = pltpu.get_barrier_semaphore()
    for facet in [partner] + others:
        pl.semaphore_signal(barrier, inc=1, device_id={"facet": facet}, device_id_type=MESH)
    for column in columns:
        pl.semaphore_signal(barrier, inc=1, device_id={"sub": column}, device_id_type=MESH)
    pl.semaphore_wait(barrier, 1 + len(others) + len(columns))


def send(src, dst, send_sem, recv_sem, **where):
    return pltpu.make_async_remote_copy(
        src_ref=src,
        dst_ref=dst,
        send_sem=send_sem,
        recv_sem=recv_sem,
        device_id=where,
        device_id_type=MESH,
    )


def gather_kernel(n, ns, with_offsets, *refs):
    if with_offsets:
        x_ref, o_ref, out_ref, offs_ref, s1, r1, s2, r2, s3, r3 = refs
    else:
        x_ref, out_ref, s1, r1, s2, r2 = refs
    me, z, core, chip, partner, others, sources, columns = peers(n, ns)
    greet(partner, others, columns if with_offsets else [])
    first = []
    for d, other in enumerate(others):
        copy = send(x_ref, out_ref.at[me], s1.at[d + 1], r1.at[d + 1], facet=other)
        copy.start()
        first.append(copy)
    near = send(x_ref, out_ref.at[me], s1.at[0], r1.at[0], facet=partner)
    near.start()
    small = []
    if with_offsets:
        for d, column in enumerate(columns):
            copy = send(o_ref, offs_ref.at[z], s3.at[d], r3.at[d], sub=column)
            copy.start()
            small.append(copy)
        offs_ref[z] = o_ref[...]
    out_ref[me] = x_ref[...]
    second = []
    for d, source in enumerate(sources):
        send(x_ref, out_ref.at[source], s1.at[d + 1], r1.at[d + 1], facet=others[d]).wait_recv()
        copy = send(out_ref.at[source], out_ref.at[source], s2.at[d], r2.at[d], facet=partner)
        copy.start()
        second.append(copy)
    partner_core = 1 - core
    send(x_ref, out_ref.at[partner], s1.at[0], r1.at[0], facet=partner).wait_recv()
    for d, source in enumerate(sources):
        twin = source - core + partner_core
        send(out_ref.at[twin], out_ref.at[twin], s2.at[d], r2.at[d], facet=partner).wait_recv()
    if with_offsets:
        for d in range(ns - 1):
            source = lax.rem(z - d - 1 + ns, ns)
            send(o_ref, offs_ref.at[source], s3.at[d], r3.at[d], sub=columns[d]).wait_recv()
    for copy in first + [near] + second + small:
        copy.wait_send()


def gather(x, offsets, n, ns, collective_id):
    with_offsets = offsets is not None
    dma = pltpu.SemaphoreType.DMA
    operands = (x, offsets) if with_offsets else (x,)
    shapes = [jax.ShapeDtypeStruct((n,) + x.shape, x.dtype)]
    sems = [dma((n // 2,)), dma((n // 2,)), dma((n // 2,)), dma((n // 2,))]
    if with_offsets:
        shapes.append(jax.ShapeDtypeStruct((ns,) + offsets.shape, offsets.dtype))
        sems += [dma((ns,)), dma((ns,))]
    return pl.pallas_call(
        functools.partial(gather_kernel, n, ns, with_offsets),
        out_shape=tuple(shapes),
        in_specs=[pl.BlockSpec(memory_space=VMEM)] * len(operands),
        out_specs=tuple([pl.BlockSpec(memory_space=VMEM)] * len(shapes)),
        scratch_shapes=sems,
        compiler_params=pltpu.CompilerParams(collective_id=collective_id, has_side_effects=True),
        name="gather_sections",
    )(*operands)


def adjoint_kernel(n, ns, part_ref, out_ref, near_buf, send_buf, far_buf, ss1, rs1, ss2, rs2, sl, sr, rz):
    me, z, core, chip, partner, others, sources, columns = peers(n, ns)
    half = n // 2
    greet(partner, others, columns)
    partner_core = 1 - core
    order = list(range(1, half)) + [0]
    near = {}
    for d in order:
        dest = lax.rem(chip + d, half) * 2 + partner_core
        copy = send(part_ref.at[dest], near_buf.at[d], ss1.at[d], rs1.at[d], facet=partner)
        copy.start()
        near[d] = copy
    far = []
    for d in range(1, half):
        dest = lax.rem(chip + d, half) * 2 + core
        near[d].wait_recv()
        send_buf[d] = (part_ref[dest].astype(F32) + near_buf[d].astype(F32)).astype(BF16)
        copy = send(send_buf.at[d], far_buf.at[d], ss2.at[d], rs2.at[d], facet=dest)
        copy.start()
        far.append(copy)
    near[0].wait_recv()
    total = part_ref[me].astype(F32) + near_buf[0].astype(F32)
    for d in range(1, half):
        far[d - 1].wait_recv()
        total += far_buf[d].astype(F32)
    out_ref[z] = total.astype(BF16)
    rows = out_ref.shape[1] // CHUNKS

    def hop(source, k, right):
        piece = out_ref.at[source, pl.ds(k * rows, rows)]
        sem = sr if right else sl
        to = z + 1 if right else z - 1
        return send(piece, piece, sem.at[source, k], rz.at[source, k], sub=to)

    for k in range(CHUNKS):

        @pl.when(z < ns - 1)
        def _():
            hop(z, k, True).start()

        @pl.when(z > 0)
        def _():
            hop(z, k, False).start()

    for d in range(1, ns):
        for k in range(CHUNKS):

            @pl.when(z - d >= 0)
            def _():
                hop(z - d, k, True).wait_recv()

                @pl.when(z < ns - 1)
                def _():
                    hop(z - d, k, True).start()

            @pl.when(z + d < ns)
            def _():
                hop(z + d, k, False).wait_recv()

                @pl.when(z > 0)
                def _():
                    hop(z + d, k, False).start()

    for copy in list(near.values()) + far:
        copy.wait_send()
    for d in range(0, ns):
        for k in range(CHUNKS):

            @pl.when((z - d >= 0) & (z < ns - 1))
            def _():
                hop(z - d, k, True).wait_send()

            @pl.when((z + d < ns) & (z > 0))
            def _():
                hop(z + d, k, False).wait_send()


def adjoint(part, n, ns, collective_id):
    dma = pltpu.SemaphoreType.DMA
    half = n // 2
    block = part.shape[1:]
    return pl.pallas_call(
        functools.partial(adjoint_kernel, n, ns),
        out_shape=jax.ShapeDtypeStruct((ns,) + block, BF16),
        in_specs=[pl.BlockSpec(memory_space=VMEM)],
        out_specs=pl.BlockSpec(memory_space=VMEM),
        scratch_shapes=[
            VMEM((half,) + block, BF16),
            VMEM((half,) + block, BF16),
            VMEM((half,) + block, BF16),
            dma((half,)),
            dma((half,)),
            dma((half,)),
            dma((half,)),
            dma((ns, CHUNKS)),
            dma((ns, CHUNKS)),
            dma((ns, CHUNKS)),
        ],
        compiler_params=pltpu.CompilerParams(collective_id=collective_id, has_side_effects=True),
        name="adjoint_exchange",
    )(part)


def subgrid_kernel(
    norm, count_ref, y_ref, zb_ref, zc_ref, pos_ref, obs_ref, wt_ref, part_ref, res_ref, e_t, z_t, grid_t, acc
):
    n, _, rows = y_ref.shape
    fine = zc_ref.shape[0]
    cc, cs = zc_ref[:, :SGW], zc_ref[:, SGW:]
    for f in range(n):
        base = f * 2 * rows
        yr, yi = y_ref[f, :SGW, :], y_ref[f, SGW:, :]
        e_t[:SGW, base : base + rows] = yr
        e_t[:SGW, base + rows : base + 2 * rows] = yi
        e_t[SGW:, base : base + rows] = yi
        e_t[SGW:, base + rows : base + 2 * rows] = -yr
        for h in range(rows // fine):
            bc, bs = zb_ref[f, h : h + 1, :SGW], zb_ref[f, h : h + 1, SGW:]
            z_t[pl.ds(base + h * fine, fine), :] = (bc * cc - bs * cs).astype(BF16)
            z_t[pl.ds(base + rows + h * fine, fine), :] = (bc * cs + bs * cc).astype(BF16)
    grid_t[...] = (norm * jnp.dot(e_t[...], z_t[...], preferred_element_type=F32)).astype(BF16)
    acc[...] = jnp.zeros_like(acc)
    cells = lax.broadcasted_iota(jnp.int32, (SGW, VB), 0).astype(F32) + 0.5
    lanes = lax.broadcasted_iota(jnp.int32, (1, VB), 1)
    count = count_ref[0, 0]

    def kernel_of(position):
        distance = cells - position.astype(F32) * (1.0 / OS)
        square = distance * distance
        return jnp.where(square <= float(KSUP * KSUP), jnp.exp(-0.5 * square), 0.0).astype(BF16)

    def block(i, carry):
        start = pl.multiple_of(i * VB, VB)
        part = pl.ds(start, VB)
        ku = kernel_of(pos_ref[0:1, part])
        kv = kernel_of(pos_ref[1:2, part]).astype(F32)
        h = jnp.dot(grid_t[...], ku, preferred_element_type=F32)
        pr = jnp.sum(h[:SGW] * kv, axis=0, keepdims=True)
        pi = jnp.sum(h[SGW:] * kv, axis=0, keepdims=True)
        live = lanes + start < count
        weight = wt_ref[0:1, part].astype(F32)
        rr = jnp.where(live, weight * (obs_ref[0:1, part].astype(F32) - pr), 0.0)
        ri = jnp.where(live, weight * (obs_ref[1:2, part].astype(F32) - pi), 0.0)
        res_ref[0:1, part] = rr
        res_ref[1:2, part] = ri
        weighted = jnp.concatenate([(rr * kv).astype(BF16), (ri * kv).astype(BF16)], axis=0)
        acc[...] += lax.dot_general(ku, weighted, (((1,), (1,)), ((), ())), preferred_element_type=F32)
        return carry

    lax.fori_loop(0, pos_ref.shape[1] // VB, block, 0)
    gridded = acc[...].astype(BF16)
    for f in range(n):
        back = jnp.dot(z_t[pl.ds(f * 2 * rows, 2 * rows), :], gridded, preferred_element_type=F32)
        part_ref[f, :, :SGW] = (back[:rows, :SGW] - back[rows:, SGW:]).astype(BF16)
        part_ref[f, :, SGW:] = (back[:rows, SGW:] + back[rows:, :SGW]).astype(BF16)


def subgrid(count, y, zb, zc, positions, observed, weight, norm):
    n, _, rows = y.shape
    slots = positions.shape[1]
    vmem = pl.BlockSpec(memory_space=VMEM)
    return pl.pallas_call(
        functools.partial(subgrid_kernel, norm),
        out_shape=(
            jax.ShapeDtypeStruct((n, rows, 2 * SGW), BF16),
            jax.ShapeDtypeStruct((2, slots), F32),
        ),
        in_specs=[pl.BlockSpec(memory_space=pltpu.SMEM)] + [vmem] * 6,
        out_specs=(vmem, vmem),
        scratch_shapes=[
            VMEM((2 * SGW, n * 2 * rows), BF16),
            VMEM((n * 2 * rows, SGW), BF16),
            VMEM((2 * SGW, SGW), BF16),
            VMEM((SGW, 2 * SGW), F32),
        ],
        name="subgrid",
    )(count, y, zb, zc, positions, observed, weight)


def update_kernel(norm, step_ref, s_ref, a_ref, d_ref, st_ref):
    ns = a_ref.shape[0]
    rev = (
        lax.broadcasted_iota(jnp.int32, (SGW, SGW), 0) + lax.broadcasted_iota(jnp.int32, (SGW, SGW), 1) == SGW - 1
    ).astype(F32).astype(BF16)

    def toeplitz(c, i):
        wide = jnp.broadcast_to(d_ref[c, i : i + 1, :], (SGW, 2 * SGW))
        return pltpu.roll(wide, 0, 1, stride=1, stride_axis=0)[:, :SGW]

    def mm(a, b):
        return jnp.dot(a, b, preferred_element_type=F32)

    sr = jnp.zeros((s_ref.shape[0], SGW), F32)
    si = jnp.zeros((s_ref.shape[0], SGW), F32)
    for c in range(ns):
        ar, ai = a_ref[c, :, :SGW], a_ref[c, :, SGW:]
        vr, vi = mm(ar, rev).astype(BF16), mm(ai, rev).astype(BF16)
        d1r, d1i = toeplitz(c, 0).astype(BF16), toeplitz(c, 1).astype(BF16)
        d2r, d2i = toeplitz(c, 2).astype(BF16), toeplitz(c, 3).astype(BF16)
        sr += mm(ar, d1r) - mm(ai, d1i) + mm(vr, d2r) + mm(vi, d2i)
        si += mm(ar, d1i) + mm(ai, d1r) + mm(vr, d2i) - mm(vi, d2r)
    scale = step_ref[0, 0] * (0.5 * norm)
    st_ref[:SGW, :] = (s_ref[:, :SGW] + scale * sr).T.astype(BF16)
    st_ref[SGW:, :] = (s_ref[:, SGW:] + scale * si).T.astype(BF16)


def update(step, s, a, d, norm):
    vmem = pl.BlockSpec(memory_space=VMEM)
    return pl.pallas_call(
        functools.partial(update_kernel, norm),
        out_shape=jax.ShapeDtypeStruct((2 * SGW, s.shape[0]), BF16),
        in_specs=[pl.BlockSpec(memory_space=pltpu.SMEM)] + [vmem] * 3,
        out_specs=vmem,
        name="next_section",
    )(step, s, a, d)


def image_kernel(norm, steps_ref, model_ref, a0_ref, a1_ref, tw_ref, bt_ref, ct_ref, out_ref, turned, table):
    ns, rows, _ = a0_ref.shape
    blocks = model_ref.shape[1] // STEP
    s0, s1 = steps_ref[0, 0] * norm, steps_ref[0, 1] * norm
    fine = ct_ref.shape[2]
    for c in range(ns):
        a = s0 * a0_ref[c].astype(F32) + s1 * a1_ref[c].astype(F32)
        ar, ai = a[:, :SGW], a[:, SGW:]
        base = c * 2 * SGW
        for j in range(blocks):
            tc, ts = tw_ref[c, j : j + 1, :SGW], tw_ref[c, j : j + 1, SGW:]
            part = pl.ds(j * rows, rows)
            turned[part, base : base + SGW] = (ar * tc - ai * ts).astype(BF16)
            turned[part, base + SGW : base + 2 * SGW] = (ar * ts + ai * tc).astype(BF16)
        cc, cs = ct_ref[c, :SGW, :], ct_ref[c, SGW:, :]
        for h in range(STEP // fine):
            bc = bt_ref[c, :SGW, h : h + 1]
            bs = bt_ref[c, SGW:, h : h + 1]
            part = slice(h * fine, (h + 1) * fine)
            table[base : base + SGW, part] = (bc * cc - bs * cs).astype(BF16)
            table[base + SGW : base + 2 * SGW, part] = (-(bc * cs + bs * cc)).astype(BF16)
    width = 256

    def chunk(i, carry):
        first = pl.multiple_of(i * width, width)
        got = jnp.dot(turned[...], table[:, pl.ds(first, width)], preferred_element_type=F32)
        for j in range(blocks):
            where = pl.ds(pl.multiple_of(j * STEP + i * width, width), width)
            out_ref[:, where] = model_ref[:, where] + got[j * rows : (j + 1) * rows]
        return carry

    lax.fori_loop(0, STEP // width, chunk, 0)


def image(steps, model, a0, a1, tw, bt, ct, norm):
    ns, rows, _ = a0.shape
    vmem = pl.BlockSpec(memory_space=VMEM)
    blocks = model.shape[1] // STEP
    return pl.pallas_call(
        functools.partial(image_kernel, norm),
        out_shape=jax.ShapeDtypeStruct(model.shape, F32),
        in_specs=[pl.BlockSpec(memory_space=pltpu.SMEM)] + [vmem] * 6,
        out_specs=vmem,
        scratch_shapes=[
            VMEM((blocks * rows, ns * 2 * SGW), BF16),
            VMEM((ns * 2 * SGW, STEP), BF16),
        ],
        name="image",
    )(steps, model, a0, a1, tw, bt, ct)


def local(model_image, step_sizes, facet_offsets, col_offsets, row_offsets, counts, vis_uv, vis_obs, vis_weight):
    n = lax.axis_size("facet")
    ns = lax.axis_size("sub")
    model = model_image[0]
    rows, width = model.shape
    norm = 1.0 / math.sqrt(n * rows * width)
    me = lax.axis_index("facet")
    cells = jnp.arange(SGW, dtype=jnp.int32)
    fine = 32
    blocks = width // STEP
    pixel = facet_offsets[1, me]
    own = col_offsets[0] + cells
    coarse_pixels = pixel + fine * jnp.arange(STEP // fine, dtype=jnp.int32)
    b = cis(own[None, :], coarse_pixels[:, None])
    c = cis(own[None, :], jnp.arange(fine, dtype=jnp.int32)[:, None])
    block_starts = STEP * jnp.arange(blocks, dtype=jnp.int32)
    tw = cis(own[None, :], block_starts[:, None])[:, None, :]
    row_fine = 16
    row_q = row_offsets[0, me] + cells
    row_pixels = facet_offsets[0][:, None] + row_fine * jnp.arange(rows // row_fine, dtype=jnp.int32)[None, :]
    zb = cis(row_q[None, None, :], row_pixels[:, :, None])
    zc = cis(row_q[None, :], jnp.arange(row_fine, dtype=jnp.int32)[:, None])

    positions = vis_uv[:, 0, 0]
    observed = vis_obs[:, 0, 0]
    weight = vis_weight[0]
    count = lax.dynamic_slice(counts, (jnp.int32(0), me), (1, 1))
    steps = step_sizes[None, :]

    s0, st0 = section(model, b, c, tw, norm)
    offsets = jnp.broadcast_to(col_offsets[:, None], (8, 128))
    gathered, columns = gather(st0, offsets, n, ns, 0)
    columns = columns[:, 0, 0]
    part, _ = subgrid(count, gathered, zb, zc, positions, observed, weight, norm)

    lags = jnp.arange(2 * SGW, dtype=jnp.int32)
    lags = jnp.where(lags < SGW, lags, lags - 2 * SGW)[None, :]
    d1 = dirichlet((columns - col_offsets[0])[:, None] - lags, pixel, width)
    d2 = dirichlet(-((columns + col_offsets[0])[:, None] + SGW - 1 + lags), pixel, width)
    d = jnp.stack([d1[0], d1[1], d2[0], d2[1]], axis=1)

    a0 = adjoint(part, n, ns, 1)
    st1 = update(steps, s0, a0, d, norm)
    (gathered,) = gather(st1, None, n, ns, 2)
    part, residual = subgrid(count, gathered, zb, zc, positions, observed, weight, norm)
    a1 = adjoint(part, n, ns, 1)

    every = columns[:, None] + cells[None, :]
    lane_fine = 128
    twa = cis(every[:, None, :], block_starts[None, :, None])
    bt_pixels = pixel + lane_fine * jnp.arange(STEP // lane_fine, dtype=jnp.int32)
    every = every[:, :, None]

    def stacked(pixels):
        angles = ((every * pixels) & (NIMG - 1)).astype(F32) * (two_pi / NIMG)
        return jnp.concatenate([jnp.cos(angles), jnp.sin(angles)], axis=1)

    bt = stacked(bt_pixels[None, None, :])
    ct = stacked(jnp.arange(lane_fine, dtype=jnp.int32)[None, None, :])
    out = image(steps, model, a0, a1, twa, bt, ct, norm)
    return (out[None], residual.reshape(2, 1, 1, residual.shape[1]))


def solution(mesh):
    in_specs = (
        P("facet", None, None),
        P(),
        P(),
        P("sub"),
        P("sub", None),
        P("sub", None),
        P(None, "sub", "facet", None),
        P(None, "sub", "facet", None),
        P("sub", "facet", None),
    )
    out_specs = (P("facet", None, None), P(None, "sub", "facet", None))
    return jax.shard_map(local, mesh=mesh, in_specs=in_specs, out_specs=out_specs, check_vma=False)
```

time: 422 us -> 145 us (0.34)
  waiting for transfers between devices: 288 us -> 0 us
  Pallas kernels: 0 us -> 121 us
  other arithmetic: 69.4 us -> 11.6 us
  matrix products: 34.6 us -> 0 us
  between operations: 16.9 us -> 2.08 us
    psum x2 -> x0, waiting for transfers between devices: 170 us -> none  [local(): lax.psum(partial_gradient.astype(jnp.bfloat16), 'sub').astype(jnp.float32)]
    pallas_call x0 -> x9, Pallas kernels: none -> 121 us  [the longest x2 48.1 us: adjoint(): pl.pallas_call(functools.partial(adjoint_kernel, n, ns), out_shape=jax.Sh...]
    all_gather x4 -> x0, waiting for transfers between devices: 118 us -> none  [the longest x2 76.8 us: local(): add_pieces = lax.all_gather(gridded_bf[None], 'facet', axis=0, tiled=True)]
    another operation x9 -> x1, other arithmetic: 53.9 us -> 0.65 us  [local(): d = jnp.stack([d1[0], d1[1], d2[0], d2[1]], axis=1)]
    dot_general x16 -> x0, matrix products: 34.6 us -> none  [the longest x2 12.9 us: local(): lax.dot_general(adjoint_rows, columns_factor, (((1,), (1,)), ((), ())), p...]
    broadcast_in_dim x1 -> x0, other arithmetic: 5.81 us -> none  [local(): return (model_now[None], residual.reshape(2, 1, 1, VCAP))]
    select_n x7 -> x1, other arithmetic: 4.31 us -> 0.01 us  [local(): lags = jnp.where(lags < SGW, lags, lags - 2 * SGW)[None, :]]
    concatenate x0 -> x8, other arithmetic: none -> 4.27 us  [the longest x6 3.18 us: cis(): return jnp.concatenate([jnp.cos(angles), jnp.sin(angles)], axis=-1)]
  transfers between devices with their start and end apart: 6 -> 0, of which waited for: 6 -> 0; matrix products, arithmetic and copies ran while one was open for 3% -> 0% of each run, Pallas kernels for 0% -> 0%
where the time goes in v1:
time: 145 us; the launch traced here: 144 us
  Pallas kernels  121 us (83%)
  other arithmetic  11.6 us (8%)
  local copies, waits for them, and re-layouts  8.75 us (6%)
  between operations  2.08 us (1%)
    pallas_call x2, Pallas kernels, adjoint(): pl.pallas_call(functools.partial(adjoint_kernel, n, ns), out_shape=jax.Sh...  48.1 us
    pallas_call x2, Pallas kernels, gather(): pl.pallas_call(functools.partial(gather_kernel, n, ns, with_offsets), out...  27.2 us
    pallas_call x2, Pallas kernels, subgrid(): pl.pallas_call(functools.partial(subgrid_kernel, norm), out_shape=(jax.Sh...  22 us
    pallas_call x1, Pallas kernels, image(): pl.pallas_call(functools.partial(image_kernel, norm), out_shape=jax.Shape...  14.1 us
    pallas_call x1, Pallas kernels, section(): pl.pallas_call(functools.partial(section_kernel, norm), grid=(width // ST...  7.11 us
    concatenate x6, other arithmetic, cis(): return jnp.concatenate([jnp.cos(angles), jnp.sin(angles)], axis=-1)  3.18 us
    pallas_call x1, Pallas kernels, update(): pl.pallas_call(functools.partial(update_kernel, norm), out_shape=jax.Shap...  3 us

profile of v1, /device:TPU:0, one launch (start us, length us, event | category | flops | bytes accessed | tf_op | source)
XLA Modules:
  0.0 143.9 jit_solution(10670615036749837273)
XLA Ops:
  0.6 0.0 copy-start
  1.3 0.0 copy-done
  1.3 0.6 constant_dynamic-slice_fusion.2.count_ref
  1.9 0.7 slice_bitcast_fusion
  2.6 1.3 constant_dynamic-slice_fusion
  4.5 0.7 multiply_add_fusion
  5.2 0.7 multiply_add_fusion.1
  5.8 0.7 iota_add_fusion.1
  6.5 0.1 broadcast_add_fusion
  6.6 0.6 broadcast_in_dim.23.refs_1_
  7.2 0.1 fusion.15
  7.3 0.6 broadcast_in_dim.22.tw_ref
  7.9 1.4 copy.17
  9.3 0.1 fusion.13
  9.4 0.6 pad_maximum_fusion.6.zc_ref
  10.0 0.3 fusion.3
  10.3 0.7 pad_maximum_fusion.1.zb_ref
  11.0 0.3 fusion.9
  11.3 0.6 pad_maximum_fusion.3.c_ref
  11.9 0.6 pad_maximum_fusion.2.b_ref
  12.5 7.1 %section.1 = (f32[128,512]{1,0:T(8,128)}, bf16[512,128]{1,0:T(8,128)(2,1)}) custom-call(f32[128,8192]{1,0:T(8,128)} %bitcast.17, f32[32,512]{1,0:T(8,128)} %pad_maximum_fusion.2.b_ref, f32[32,512]{1,0:T(8,128)} %pad_maximum_fusion.3.c_ref, f32[8,1,512]{2,1,0:T(1,128)} %broadcast_in_dim.22.tw_ref), custom_call_target="tpu_custom_call" | custom-call | tf_op jit(solution)/shard_map/section/pallas_call | solution.py:71
  19.7 15.9 %gather_sections.2 = (bf16[8,512,128]{2,1,0:T(8,128)(2,1)}, s32[4,8,128]{2,1,0:T(8,128)}) custom-call(bf16[512,128]{1,0:T(8,128)(2,1)} %get-tuple-element.9.refs_0_, s32[8,128]{1,0:T(8,128)} %broadcast_in_dim.23.refs_1_), custom_call_target="tpu_custom_call" | custom-call | tf_op jit(solution)/shard_map/gather_sections/pallas_call | solution.py:175
  35.5 0.9 slice_reduce_fusion
  36.4 0.1 iota_add_fusion
  36.5 1.5 %cosine_multiply_fusion.1 = (f32[4,1,512]{2,1,0:T(1,128)S(1)}, f32[4,1,512]{2,1,0:T(1,128)S(1)}, f32[4,1,512]{2,1,0:T(1,128)S(1)}, f32[4,1,512]{2,1,0:T(1,128)S(1)}) fusion(s32[512]{0:T(512)S(1)} %compare_select_fusion, s32[4]{0:T(128)S(1)} %get-tuple-element.46, s32[]{:T(128)S(6)} %sub.64, s32[4]{0:T(128)S(1)} %get-tuple-element.47), kind=kLoop, calls=%fused_computation.37 | loop fusion | flops 88064 | bytes 34852 | tf_op jit(solution)/shard_map/mul | solution.py:41
  38.0 0.7 pad_maximum_fusion.7.d_ref
  38.6 10.9 %subgrid.2 = (bf16[8,128,512]{2,1,0:T(8,128)(2,1)}, f32[2,4096]{1,0:T(2,128)}) custom-call(s32[1,1]{1,0:T(1,128)} %constant_dynamic-slice_fusion.2.count_ref, bf16[8,512,128]{2,1,0:T(8,128)(2,1)} %get-tuple-element.10.y_ref, f32[8,8,512]{2,1,0:T(8,128)} %pad_maximum_fusion.1.zb_ref, f32[16,512]{1,0:T(8,128)} %pad_maximum_fusion.6.zc_ref, ...), custom_call_target="tpu_custom_call" | custom-call | tf_op jit(solution)/shard_map/subgrid/pallas_call | solution.py:347
  49.5 24.3 %adjoint_exchange.2.a_ref.a0_ref = bf16[4,128,512]{2,1,0:T(8,128)(2,1)} custom-call(bf16[8,128,512]{2,1,0:T(8,128)(2,1)} %get-tuple-element.11.part_ref), custom_call_target="tpu_custom_call" | custom-call | tf_op jit(solution)/shard_map/adjoint_exchange/pallas_call | solution.py:267
  73.8 3.0 %next_section.1.refs_0_ = bf16[512,128]{1,0:T(8,128)(2,1)} custom-call(f32[1,2]{1,0:T(1,128)} %bitcast.27, f32[128,512]{1,0:T(8,128)} %get-tuple-element.12.s_ref, bf16[4,128,512]{2,1,0:T(8,128)(2,1)} %adjoint_exchange.2.a_ref.a0_ref, f32[4,4,512]{2,1,0:T(4,128)} %pad_maximum_fusion.7.d_ref), custom_call_target="tpu_custom_call" | custom-call | tf_op jit(solution)/shard_map/next_section/pallas_call | solution.py:394
  76.8 0.2 fusion.5
  77.0 0.2 fusion.7
  77.2 0.6 pad_maximum_fusion.4.tw_ref
  77.9 11.3 %gather_sections.3.y_ref = bf16[8,512,128]{2,1,0:T(8,128)(2,1)} custom-call(bf16[512,128]{1,0:T(8,128)(2,1)} %next_section.1.refs_0_), custom_call_target="tpu_custom_call" | custom-call | tf_op jit(solution)/shard_map/gather_sections/pallas_call | solution.py:175
  89.2 11.1 %subgrid.3 = (bf16[8,128,512]{2,1,0:T(8,128)(2,1)}, f32[2,4096]{1,0:T(2,128)}) custom-call(s32[1,1]{1,0:T(1,128)} %constant_dynamic-slice_fusion.2.count_ref, bf16[8,512,128]{2,1,0:T(8,128)(2,1)} %gather_sections.3.y_ref, f32[8,8,512]{2,1,0:T(8,128)} %pad_maximum_fusion.1.zb_ref, f32[16,512]{1,0:T(8,128)} %pad_maximum_fusion.6.zc_ref, s32[2,4096]{1,0:T(2,128)} %bitcast.21, ...), custom_call_target="tpu_custom_call" | custom-call | tf_op jit(solution)/shard_map/subgrid/pallas_call | solution.py:347
  100.3 23.8 %adjoint_exchange.3.a1_ref = bf16[4,128,512]{2,1,0:T(8,128)(2,1)} custom-call(bf16[8,128,512]{2,1,0:T(8,128)(2,1)} %get-tuple-element.14.part_ref), custom_call_target="tpu_custom_call" | custom-call | tf_op jit(solution)/shard_map/adjoint_exchange/pallas_call | solution.py:267
  124.0 1.4 copy.14
  125.5 1.3 copy.13.bt_ref
  126.8 1.9 %fusion.1 = (f32[4,256,128]{2,1,0:T(8,128)S(1)}, f32[4,256,128]{2,1,0:T(8,128)S(1)}) fusion(s32[4,256]{1,0:T(4,128)S(1)} %iota_add_fusion), kind=kLoop, calls=%fused_computation.3 | loop fusion | flops 524288 | bytes 1052672 | tf_op jit(solution)/shard_map/cos | solution.py:509
  128.7 1.1 pad_maximum_fusion.ct_ref
  129.8 14.1 %image.1 = f32[128,8192]{1,0:T(8,128)} custom-call(f32[1,2]{1,0:T(1,128)} %bitcast.28, f32[128,8192]{1,0:T(8,128)} %bitcast.18, bf16[4,128,512]{2,1,0:T(8,128)(2,1)} %adjoint_exchange.2.a_ref.a0_ref, bf16[4,128,512]{2,1,0:T(8,128)(2,1)} %adjoint_exchange.3.a1_ref, f32[4,8,512]{2,1,0:T(8,128)} %pad_maximum_fusion.4.tw_ref, f32[4,512,8]{2,1,0:T(8,128)} %copy.13.bt_ref, ...), custom_call_target="tpu_custom_call" | custom-call | tf_op jit(solution)/shard_map/image/pallas_call | solution.py:441
  (7 shorter events, 0.0 us)
Async XLA Ops:
  0.6 0.7 copy-start

commit v2 on v0

v2 whole, which is shorter than its diff:
```python
import functools
import math

import jax
import jax.numpy as jnp
from jax import lax
from jax.experimental import pallas as pl
from jax.experimental.pallas import tpu as pltpu
from jax.sharding import PartitionSpec as P

NIMG = 65536
SGW = 256
VB = 512
OS = 8
KSUP = 4
ITERS = 2
STEP = 1024
CHUNKS = 4
MESH = pl.DeviceIdType.MESH
VMEM = pltpu.VMEM
F32 = jnp.float32
BF16 = jnp.bfloat16
two_pi = 2.0 * math.pi


def iota(shape, dim):
    return lax.broadcasted_iota(jnp.int32, shape, dim)


def cis(frequency, pixels):
    index = (frequency * pixels) & (NIMG - 1)
    angles = index.astype(F32) * (two_pi / NIMG)
    return jnp.cos(angles), jnp.sin(angles)


def dirichlet(k, start, length):
    k = ((k + NIMG // 2) & (NIMG - 1)) - NIMG // 2
    half = math.pi / NIMG
    phase = ((k * (2 * start + length - 1)) & (2 * NIMG - 1)).astype(F32) * half
    top = jnp.sin(((k * length) & (2 * NIMG - 1)).astype(F32) * half)
    bottom = jnp.sin(k.astype(F32) * half)
    zero = k == 0
    ratio = jnp.where(zero, float(length), top / jnp.where(zero, 1.0, bottom))
    phase = jnp.where(zero, 0.0, phase)
    return ratio * jnp.cos(phase), ratio * jnp.sin(phase)


def mm(a, b):
    return jnp.dot(a, b, preferred_element_type=F32)


def peers(n, ns):
    me = lax.axis_index("facet")
    z = lax.axis_index("sub")
    core = lax.rem(me, 2)
    chip = me // 2
    partner = me + 1 - 2 * core
    others = [lax.rem(chip + d, n // 2) * 2 + core for d in range(1, n // 2)]
    sources = [lax.rem(chip - d + n // 2, n // 2) * 2 + core for d in range(1, n // 2)]
    columns = [lax.rem(z + d, ns) for d in range(1, ns)]
    return me, z, core, chip, partner, others, sources, columns


def greet(partner, others, columns):
    barrier = pltpu.get_barrier_semaphore()
    for facet in [partner] + others:
        pl.semaphore_signal(barrier, inc=1, device_id={"facet": facet}, device_id_type=MESH)
    for column in columns:
        pl.semaphore_signal(barrier, inc=1, device_id={"sub": column}, device_id_type=MESH)
    pl.semaphore_wait(barrier, 1 + len(others) + len(columns))


def send(src, dst, send_sem, recv_sem, **where):
    return pltpu.make_async_remote_copy(
        src_ref=src,
        dst_ref=dst,
        send_sem=send_sem,
        recv_sem=recv_sem,
        device_id=where,
        device_id_type=MESH,
    )


def step_kernel(
    n, ns, steps_ref, facet_ref, col_ref, row_ref, count_ref, model_ref, pos_ref, obs_ref, wt_ref,
    out_ref, res_ref,
    mb, table, s_ref, st, got_y, o_ref, offs, z_t, gacc, grid_t, ku_t, kv_t, acc, part_p, part_o,
    near_buf, send_buf, far_buf, adj, lag_t, tw_t, image_t, turned,
    ms, s1, r1, s2, r2, s3, r3, ss1, rs1, ss2, rs2, sl, sr, rz,
):
    rows, width = out_ref.shape
    blocks = width // STEP
    slots = pos_ref.shape[-1]
    half = n // 2
    norm = 1.0 / math.sqrt(n * rows * width)
    me, z, core, chip, partner, others, sources, columns = peers(n, ns)
    partner_core = 1 - core
    pixel = facet_ref[1, me]
    own = col_ref[0]

    loads = []
    for j in range(blocks):
        where = pl.ds(j * STEP, STEP)
        load = pltpu.make_async_copy(model_ref.at[:, where], out_ref.at[:, where], ms.at[j])
        load.start()
        loads.append(load)
    o_ref[...] = jnp.full(o_ref.shape, own, jnp.int32)

    fine = 32
    q = iota((fine, SGW), 1) + own
    bc, bs = cis(q, pixel + fine * iota((STEP // fine, SGW), 0))
    cc, cs = cis(q, iota((fine, SGW), 0))
    for h in range(STEP // fine):
        hc, hs = bc[h : h + 1], bs[h : h + 1]
        table[h * fine : (h + 1) * fine, :SGW] = (hc * cc - hs * cs).astype(BF16)
        table[h * fine : (h + 1) * fine, SGW:] = (-(hc * cs + hs * cc)).astype(BF16)
    tc, ts = cis(iota((blocks, SGW), 1) + own, STEP * iota((blocks, SGW), 0))
    for j in range(blocks):
        loads[j].wait()
        mb[j * rows : (j + 1) * rows, :] = out_ref[:, j * STEP : (j + 1) * STEP].astype(BF16)
    yr = jnp.zeros((rows, SGW), F32)
    yi = jnp.zeros((rows, SGW), F32)
    group = max(blocks // 2, 1)
    for first in range(0, blocks, group):
        part = mm(mb[first * rows : (first + group) * rows, :], table[...])
        for j in range(group):
            pr, pi = part[j * rows : (j + 1) * rows, :SGW], part[j * rows : (j + 1) * rows, SGW:]
            c, s = tc[first + j : first + j + 1], ts[first + j : first + j + 1]
            yr += pr * c + pi * s
            yi += pi * c - pr * s
    s_ref[:, :SGW] = yr
    s_ref[:, SGW:] = yi
    st[0, :SGW, :] = yr.T.astype(BF16)
    st[0, SGW:, :] = yi.T.astype(BF16)
    greet(partner, others, columns)

    def subgrid_tables():
        row_fine = 16
        q = iota((row_fine, SGW), 1) + row_ref[0, me]
        cc, cs = cis(q, iota((row_fine, SGW), 0))
        for f in range(n):
            steps = rows // row_fine
            bc, bs = cis(
                iota((steps, SGW), 1) + row_ref[0, me], facet_ref[0, f] + row_fine * iota((steps, SGW), 0)
            )
            for h in range(steps):
                hc, hs = bc[h : h + 1], bs[h : h + 1]
                at = h * row_fine
                z_t[f, at : at + row_fine, :] = (hc * cc - hs * cs).astype(BF16)
                z_t[f, rows + at : rows + at + row_fine, :] = (hc * cs + hs * cc).astype(BF16)
        cells = iota((SGW, VB), 0).astype(F32) + 0.5

        def kernel_of(position):
            distance = cells - position.astype(F32) * (1.0 / OS)
            square = distance * distance
            return jnp.where(square <= float(KSUP * KSUP), jnp.exp(-0.5 * square), 0.0).astype(BF16)

        def block(i, carry):
            part = pl.ds(pl.multiple_of(i * VB, VB), VB)
            ku_t[:, part] = kernel_of(pos_ref[0, 0, 0:1, part])
            kv_t[:, part] = kernel_of(pos_ref[1, 0, 0:1, part])
            return carry

        lax.fori_loop(0, slots // VB, block, 0)

    def lag_tables():
        lags = iota((1, 2 * SGW), 1)
        lags = jnp.where(lags < SGW, lags, lags - 2 * SGW)

        def column(c, carry):
            other = jnp.broadcast_to(offs[c][0:1, 0:1], (1, 2 * SGW))
            d1 = dirichlet(other - own - lags, pixel, width)
            d2 = dirichlet(-(other + own + SGW - 1 + lags), pixel, width)
            for i, line in enumerate(d1 + d2):
                wide = jnp.broadcast_to(line, (SGW, 2 * SGW))
                lag_t[c, i] = pltpu.roll(wide, 0, 1, stride=1, stride_axis=0)[:, :SGW].astype(BF16)
            return carry

        lax.fori_loop(0, ns, column, 0)

    def image_tables():
        lane_fine = 128
        coarse = STEP // lane_fine

        def column(c, carry):
            other = offs[c][0:1, 0:1]
            tc, ts = cis(iota((blocks, SGW), 1) + other, STEP * iota((blocks, SGW), 0))
            tw_t[c, :, :SGW] = tc
            tw_t[c, :, SGW:] = ts
            q = iota((SGW, lane_fine), 0) + other
            bc, bs = cis(q, pixel + lane_fine * iota((SGW, lane_fine), 1))
            cc, cs = cis(q, iota((SGW, lane_fine), 1))
            for h in range(coarse):
                hc, hs = bc[:, h : h + 1], bs[:, h : h + 1]
                part = slice(h * lane_fine, (h + 1) * lane_fine)
                image_t[c, :SGW, part] = (hc * cc - hs * cs).astype(BF16)
                image_t[c, SGW:, part] = (-(hc * cs + hs * cc)).astype(BF16)
            return carry

        lax.fori_loop(0, ns, column, 0)

    def grid_term(t, f):
        yr, yi = got_y[t, f, :SGW, :], got_y[t, f, SGW:, :]
        zf = z_t[f]
        gacc[:SGW] += mm(jnp.concatenate([yr, yi], axis=1), zf)
        gacc[SGW:] += mm(jnp.concatenate([yi, -yr], axis=1), zf)

    def gather_sections(t, meanwhile):
        sent = []
        for d, other in enumerate(others):
            copy = send(st.at[t], got_y.at[t, me], s1.at[t, d + 1], r1.at[t, d + 1], facet=other)
            copy.start()
            sent.append(copy)
        near = send(st.at[t], got_y.at[t, me], s1.at[t, 0], r1.at[t, 0], facet=partner)
        near.start()
        sent.append(near)
        small = []
        if t == 0:
            for d, column in enumerate(columns):
                copy = send(o_ref, offs.at[z], s3.at[d], r3.at[d], sub=column)
                copy.start()
                sent.append(copy)
            offs[z] = o_ref[...]
        got_y[t, me] = st[t]
        meanwhile()
        gacc[...] = jnp.zeros_like(gacc)
        grid_term(t, me)
        send(st.at[t], got_y.at[t, partner], s1.at[t, 0], r1.at[t, 0], facet=partner).wait_recv()
        grid_term(t, partner)
        for d, source in enumerate(sources):
            send(st.at[t], got_y.at[t, source], s1.at[t, d + 1], r1.at[t, d + 1], facet=others[d]).wait_recv()
            block = got_y.at[t, source]
            copy = send(block, block, s2.at[t, d], r2.at[t, d], facet=partner)
            copy.start()
            sent.append(copy)
            grid_term(t, source)
        for d, source in enumerate(sources):
            twin = source - core + partner_core
            block = got_y.at[t, twin]
            send(block, block, s2.at[t, d], r2.at[t, d], facet=partner).wait_recv()
            grid_term(t, twin)
        if t == 0:
            for d in range(ns - 1):
                source = lax.rem(z - d - 1 + ns, ns)
                send(o_ref, offs.at[source], s3.at[d], r3.at[d], sub=columns[d]).wait_recv()
        for copy in sent:
            copy.wait_send()
        grid_t[...] = (norm * gacc[...]).astype(BF16)

    def sweep(last):
        acc[...] = jnp.zeros_like(acc)
        lanes = iota((1, VB), 1)
        count = count_ref[0, me]

        def block(i, carry):
            start = pl.multiple_of(i * VB, VB)
            part = pl.ds(start, VB)
            ku = ku_t[:, part]
            kv = kv_t[:, part].astype(F32)
            h = mm(grid_t[...], ku)
            pr = jnp.sum(h[:SGW] * kv, axis=0, keepdims=True)
            pi = jnp.sum(h[SGW:] * kv, axis=0, keepdims=True)
            live = lanes + start < count
            weight = wt_ref[0, 0:1, part].astype(F32)
            rr = jnp.where(live, weight * (obs_ref[0, 0, 0:1, part].astype(F32) - pr), 0.0)
            ri = jnp.where(live, weight * (obs_ref[1, 0, 0:1, part].astype(F32) - pi), 0.0)
            if last:
                res_ref[0, 0, 0:1, part] = rr
                res_ref[1, 0, 0:1, part] = ri
            weighted = jnp.concatenate([(rr * kv).astype(BF16), (ri * kv).astype(BF16)], axis=0)
            acc[...] += lax.dot_general(ku, weighted, (((1,), (1,)), ((), ())), preferred_element_type=F32)
            return carry

        lax.fori_loop(0, slots // VB, block, 0)

    def exchange(t, meanwhile, use_column):
        gridded = acc[...].astype(BF16)

        def fold(dest):
            back = mm(z_t[dest], gridded)
            return back[:rows, :SGW] - back[rows:, SGW:], back[:rows, SGW:] + back[rows:, :SGW]

        order = list(range(1, half)) + [0]
        near = {}
        for d in order:
            real, imag = fold(lax.rem(chip + d, half) * 2 + partner_core)
            part_p[t, d, :, :SGW] = real.astype(BF16)
            part_p[t, d, :, SGW:] = imag.astype(BF16)
            near[d] = send(part_p.at[t, d], near_buf.at[t, d], ss1.at[t, d], rs1.at[t, d], facet=partner)
            near[d].start()
        for d in order:
            real, imag = fold(lax.rem(chip + d, half) * 2 + core)
            part_o[d, :, :SGW] = real
            part_o[d, :, SGW:] = imag
        far = []
        for d in range(1, half):
            dest = lax.rem(chip + d, half) * 2 + core
            near[d].wait_recv()
            send_buf[t, d] = (part_o[d] + near_buf[t, d].astype(F32)).astype(BF16)
            copy = send(send_buf.at[t, d], far_buf.at[t, d], ss2.at[t, d], rs2.at[t, d], facet=dest)
            copy.start()
            far.append(copy)
        meanwhile()
        near[0].wait_recv()
        total = part_o[0] + near_buf[t, 0].astype(F32)
        for d in range(1, half):
            far[d - 1].wait_recv()
            total += far_buf[t, d].astype(F32)
        adj[t, z] = total.astype(BF16)
        size = rows // CHUNKS

        def hop(source, k, right):
            piece = adj.at[t, source, pl.ds(k * size, size)]
            sem = sr if right else sl
            to = z + 1 if right else z - 1
            return send(piece, piece, sem.at[t, source, k], rz.at[t, source, k], sub=to)

        for k in range(CHUNKS):

            @pl.when(z < ns - 1)
            def _():
                hop(z, k, True).start()

            @pl.when(z > 0)
            def _():
                hop(z, k, False).start()

        use_column(z)
        for d in range(1, ns):
            for k in range(CHUNKS):

                @pl.when(z - d >= 0)
                def _():
                    hop(z - d, k, True).wait_recv()

                    @pl.when(z < ns - 1)
                    def _():
                        hop(z - d, k, True).start()

                @pl.when(z + d < ns)
                def _():
                    hop(z + d, k, False).wait_recv()

                    @pl.when(z > 0)
                    def _():
                        hop(z + d, k, False).start()

            @pl.when(z - d >= 0)
            def _():
                use_column(z - d)

            @pl.when(z + d < ns)
            def _():
                use_column(z + d)

        for copy in list(near.values()) + far:
            copy.wait_send()
        for d in range(0, ns):
            for k in range(CHUNKS):

                @pl.when((z - d >= 0) & (z < ns - 1))
                def _():
                    hop(z - d, k, True).wait_send()

                @pl.when((z + d < ns) & (z > 0))
                def _():
                    hop(z + d, k, False).wait_send()

    mirror = (iota((SGW, SGW), 0) + iota((SGW, SGW), 1) == SGW - 1).astype(F32).astype(BF16)

    def add_to_section(c):
        scale = steps_ref[0] * (0.5 * norm)
        ar, ai = adj[0, c, :, :SGW], adj[0, c, :, SGW:]
        vr, vi = mm(ar, mirror).astype(BF16), mm(ai, mirror).astype(BF16)
        d1r, d1i, d2r, d2i = lag_t[c, 0], lag_t[c, 1], lag_t[c, 2], lag_t[c, 3]
        s_ref[:, :SGW] += scale * (mm(ar, d1r) - mm(ai, d1i) + mm(vr, d2r) + mm(vi, d2i))
        s_ref[:, SGW:] += scale * (mm(ar, d1i) + mm(ai, d1r) + mm(vr, d2i) - mm(vi, d2r))

    def add_to_image(c):
        a = (steps_ref[0] * norm) * adj[0, c].astype(F32) + (steps_ref[1] * norm) * adj[1, c].astype(F32)
        ar, ai = a[:, :SGW], a[:, SGW:]
        for j in range(blocks):
            tc, ts = tw_t[c, j : j + 1, :SGW], tw_t[c, j : j + 1, SGW:]
            turned[j * rows : (j + 1) * rows, :SGW] = (ar * tc - ai * ts).astype(BF16)
            turned[j * rows : (j + 1) * rows, SGW:] = (ar * ts + ai * tc).astype(BF16)
        lanes = 256

        def chunk(i, carry):
            got = mm(turned[...], image_t[c, :, pl.ds(pl.multiple_of(i * lanes, lanes), lanes)])
            for j in range(blocks):
                where = pl.ds(pl.multiple_of(j * STEP + i * lanes, lanes), lanes)
                out_ref[:, where] += got[j * rows : (j + 1) * rows]
            return carry

        lax.fori_loop(0, STEP // lanes, chunk, 0)

    gather_sections(0, subgrid_tables)
    sweep(False)
    exchange(0, lag_tables, add_to_section)
    st[1, :SGW, :] = s_ref[:, :SGW].T.astype(BF16)
    st[1, SGW:, :] = s_ref[:, SGW:].T.astype(BF16)
    gather_sections(1, image_tables)
    sweep(True)
    exchange(1, lambda: None, add_to_image)


def local(model_image, step_sizes, facet_offsets, col_offsets, row_offsets, counts, vis_uv, vis_obs, vis_weight):
    n = lax.axis_size("facet")
    ns = lax.axis_size("sub")
    model = model_image[0]
    rows, width = model.shape
    slots = vis_uv.shape[-1]
    half = n // 2
    blocks = width // STEP
    dma = pltpu.SemaphoreType.DMA
    vmem = pl.BlockSpec(memory_space=VMEM)
    smem = pl.BlockSpec(memory_space=pltpu.SMEM)
    image, residual = pl.pallas_call(
        functools.partial(step_kernel, n, ns),
        out_shape=(
            jax.ShapeDtypeStruct(model.shape, F32),
            jax.ShapeDtypeStruct((2, 1, 1, slots), F32),
        ),
        in_specs=[smem] * 5 + [pl.BlockSpec(memory_space=pl.ANY)] + [vmem] * 3,
        out_specs=(vmem, vmem),
        scratch_shapes=[
            VMEM((blocks * rows, STEP), BF16),
            VMEM((STEP, 2 * SGW), BF16),
            VMEM((rows, 2 * SGW), F32),
            VMEM((ITERS, 2 * SGW, rows), BF16),
            VMEM((ITERS, n, 2 * SGW, rows), BF16),
            VMEM((8, 128), jnp.int32),
            VMEM((ns, 8, 128), jnp.int32),
            VMEM((n, 2 * rows, SGW), BF16),
            VMEM((2 * SGW, SGW), F32),
            VMEM((2 * SGW, SGW), BF16),
            VMEM((SGW, slots), BF16),
            VMEM((SGW, slots), BF16),
            VMEM((SGW, 2 * SGW), F32),
            VMEM((ITERS, half, rows, 2 * SGW), BF16),
            VMEM((half, rows, 2 * SGW), F32),
            VMEM((ITERS, half, rows, 2 * SGW), BF16),
            VMEM((ITERS, half, rows, 2 * SGW), BF16),
            VMEM((ITERS, half, rows, 2 * SGW), BF16),
            VMEM((ITERS, ns, rows, 2 * SGW), BF16),
            VMEM((ns, 4, SGW, SGW), BF16),
            VMEM((ns, blocks, 2 * SGW), F32),
            VMEM((ns, 2 * SGW, STEP), BF16),
            VMEM((blocks * rows, 2 * SGW), BF16),
            dma((blocks,)),
            dma((ITERS, half)),
            dma((ITERS, half)),
            dma((ITERS, half)),
            dma((ITERS, half)),
            dma((ns,)),
            dma((ns,)),
            dma((ITERS, half)),
            dma((ITERS, half)),
            dma((ITERS, half)),
            dma((ITERS, half)),
            dma((ITERS, ns, CHUNKS)),
            dma((ITERS, ns, CHUNKS)),
            dma((ITERS, ns, CHUNKS)),
        ],
        compiler_params=pltpu.CompilerParams(collective_id=0, has_side_effects=True),
        name="cycles",
    )(step_sizes, facet_offsets, col_offsets, row_offsets, counts, model, vis_uv, vis_obs, vis_weight)
    return (image[None], residual)


def solution(mesh):
    in_specs = (
        P("facet", None, None),
        P(),
        P(),
        P("sub"),
        P("sub", None),
        P("sub", None),
        P(None, "sub", "facet", None),
        P(None, "sub", "facet", None),
        P("sub", "facet", None),
    )
    out_specs = (P("facet", None, None), P(None, "sub", "facet", None))
    return jax.shard_map(local, mesh=mesh, in_specs=in_specs, out_specs=out_specs, check_vma=False)
```

time: 422 us -> 93.9 us (0.22)
  waiting for transfers between devices: 288 us -> 0 us
  Pallas kernels: 0 us -> 85.7 us
  other arithmetic: 69.4 us -> 0 us
  matrix products: 34.6 us -> 0 us
  between operations: 16.9 us -> 1.29 us
    psum x2 -> x0, waiting for transfers between devices: 170 us -> none  [local(): lax.psum(partial_gradient.astype(jnp.bfloat16), 'sub').astype(jnp.float32)]
    all_gather x4 -> x0, waiting for transfers between devices: 118 us -> none  [the longest x2 76.8 us: local(): add_pieces = lax.all_gather(gridded_bf[None], 'facet', axis=0, tiled=True)]
    pallas_call x0 -> x1, Pallas kernels: none -> 85.7 us  [local(): pl.pallas_call(functools.partial(step_kernel, n, ns), out_shape=(jax.Shap...]
    another operation x9 -> x0, other arithmetic: 53.9 us -> none
    dot_general x16 -> x0, matrix products: 34.6 us -> none  [the longest x2 12.9 us: local(): lax.dot_general(adjoint_rows, columns_factor, (((1,), (1,)), ((), ())), p...]
    broadcast_in_dim x1 -> x0, other arithmetic: 5.81 us -> none  [local(): return (model_now[None], residual.reshape(2, 1, 1, VCAP))]
    select_n x7 -> x0, other arithmetic: 4.31 us -> none  [the longest x4 2.85 us: block_pass(): jnp.where(is_live, weight_float * (observed[0].astype(jnp.float32) - pred...]
  transfers between devices with their start and end apart: 6 -> 0, of which waited for: 6 -> 0; matrix products, arithmetic and copies ran while one was open for 3% -> 0% of each run, Pallas kernels for 0% -> 0%
where the time goes in v2:
time: 93.9 us; the launch traced here: 93.6 us
  Pallas kernels  85.7 us (91%)
  local copies, waits for them, and re-layouts  6.59 us (7%)
  between operations  1.29 us (1%)
    pallas_call x1, Pallas kernels, local(): pl.pallas_call(functools.partial(step_kernel, n, ns), out_shape=(jax.Shap...  85.7 us
    unnamed x5, local copies, waits for them, and re-layouts  6.59 us

profile of v2, /device:TPU:0, one launch (start us, length us, event | category | flops | bytes accessed | tf_op | source)
XLA Modules:
  0.0 93.6 jit_solution(9779882082582456317)
XLA Ops:
  1.3 1.4 %copy.11.obs_ref = bf16[2,1,1,4096]{3,2,1,0:T(2,128)(2,1)} copy(bf16[2,1,1,4096]{3,0,2,1:T(2,128)(2,1)} %param.16) | data formatting | bytes 32768 | tf_op args[7]
  2.6 85.7 %cycles.1 = (f32[128,8192]{1,0:T(8,128)}, f32[2,1,1,4096]{3,2,1,0:T(1,128)}) custom-call(f32[2]{0:T(128)} %steps_ref.1, s32[2,8]{1,0:T(2,128)} %facet_ref.1, s32[1]{0:T(128)S(6)} %copy.14.col_ref, s32[1,8]{1,0:T(1,128)} %row_ref.1, s32[1,8]{1,0:T(1,128)} %count_ref.1, f32[128,8192]{1,0:T(8,128)} %bitcast.2, s32[2,1,1,4096]{3,2,1,0:T(1,128)} %pos_ref.1, ...), custom_call_target="tpu_custom_call" | custom-call | tf_op jit(solution)/shard_map/cycles/pallas_call | solution.py:418
  88.4 0.0 copy-start
  88.4 4.6 %copy.15 = f32[1,128,8192]{2,1,0:T(8,128)} copy(f32[1,128,8192]{2,1,0:T(8,128)} %bitcast.3) | data formatting | bytes 8388608
  93.0 0.0 copy-done
  93.0 0.6 copy.16
Async XLA Ops:
  88.4 4.6 %copy-start = (f32[2,1,1,4096]{3,2,1,0:T(1,128)S(1)}, f32[2,1,1,4096]{3,2,1,0:T(1,128)}, u32[]{:S(2)}) copy-start(f32[2,1,1,4096]{3,2,1,0:T(1,128)} %get-tuple-element.9) | copy-start | bytes 98308

commit v3 on v2

--- a/solution.py
+++ b/solution.py
@@ -16,6 +16,7 @@
 ITERS = 2
 STEP = 1024
 CHUNKS = 4
+VMEM_BYTES = 67043328
 MESH = pl.DeviceIdType.MESH
 VMEM = pltpu.VMEM
 F32 = jnp.float32
@@ -67,7 +68,6 @@
         pl.semaphore_signal(barrier, inc=1, device_id={"facet": facet}, device_id_type=MESH)
     for column in columns:
         pl.semaphore_signal(barrier, inc=1, device_id={"sub": column}, device_id_type=MESH)
-    pl.semaphore_wait(barrier, 1 + len(others) + len(columns))
 
 
 def send(src, dst, send_sem, recv_sem, **where):
@@ -97,6 +97,7 @@
     partner_core = 1 - core
     pixel = facet_ref[1, me]
     own = col_ref[0]
+    greet(partner, others, columns)
 
     loads = []
     for j in range(blocks):
@@ -132,7 +133,7 @@
     s_ref[:, SGW:] = yi
     st[0, :SGW, :] = yr.T.astype(BF16)
     st[0, SGW:, :] = yi.T.astype(BF16)
-    greet(partner, others, columns)
+    pl.semaphore_wait(pltpu.get_barrier_semaphore(), 1 + len(others) + len(columns))
 
     def subgrid_tables():
         row_fine = 16
@@ -163,7 +164,7 @@
 
         lax.fori_loop(0, slots // VB, block, 0)
 
-    def lag_tables():
+    def lag_tables(first, stop):
         lags = iota((1, 2 * SGW), 1)
         lags = jnp.where(lags < SGW, lags, lags - 2 * SGW)
 
@@ -176,9 +177,9 @@
                 lag_t[c, i] = pltpu.roll(wide, 0, 1, stride=1, stride_axis=0)[:, :SGW].astype(BF16)
             return carry
 
-        lax.fori_loop(0, ns, column, 0)
-
-    def image_tables():
+        lax.fori_loop(first, stop, column, 0)
+
+    def image_tables(first, stop):
         lane_fine = 128
         coarse = STEP // lane_fine
 
@@ -197,7 +198,7 @@
                 image_t[c, SGW:, part] = (-(hc * cs + hs * cc)).astype(BF16)
             return carry
 
-        lax.fori_loop(0, ns, column, 0)
+        lax.fori_loop(first, stop, column, 0)
 
     def grid_term(t, f):
         yr, yi = got_y[t, f, :SGW, :], got_y[t, f, SGW:, :]
@@ -239,10 +240,6 @@
             block = got_y.at[t, twin]
             send(block, block, s2.at[t, d], r2.at[t, d], facet=partner).wait_recv()
             grid_term(t, twin)
-        if t == 0:
-            for d in range(ns - 1):
-                source = lax.rem(z - d - 1 + ns, ns)
-                send(o_ref, offs.at[source], s3.at[d], r3.at[d], sub=columns[d]).wait_recv()
         for copy in sent:
             copy.wait_send()
         grid_t[...] = (norm * gacc[...]).astype(BF16)
@@ -263,7 +260,7 @@
             live = lanes + start < count
             weight = wt_ref[0, 0:1, part].astype(F32)
             rr = jnp.where(live, weight * (obs_ref[0, 0, 0:1, part].astype(F32) - pr), 0.0)
-            ri = jnp.where(live, weight * (obs_ref[1, 0, 0:1, part].astype(F32) - pi), 0.0)
+            ri = jnp.where(live, weight * (obs_ref[0, 0, 1:2, part].astype(F32) - pi), 0.0)
             if last:
                 res_ref[0, 0, 0:1, part] = rr
                 res_ref[1, 0, 0:1, part] = ri
@@ -292,23 +289,24 @@
             real, imag = fold(lax.rem(chip + d, half) * 2 + core)
             part_o[d, :, :SGW] = real
             part_o[d, :, SGW:] = imag
-        far = []
-        for d in range(1, half):
+        size = rows // CHUNKS
+
+        def away(d, k):
+            cut = pl.ds(k * size, size)
             dest = lax.rem(chip + d, half) * 2 + core
-            near[d].wait_recv()
-            send_buf[t, d] = (part_o[d] + near_buf[t, d].astype(F32)).astype(BF16)
-            copy = send(send_buf.at[t, d], far_buf.at[t, d], ss2.at[t, d], rs2.at[t, d], facet=dest)
-            copy.start()
-            far.append(copy)
+            return send(
+                send_buf.at[t, d, cut], far_buf.at[t, d, cut], ss2.at[t, d, k], rs2.at[t, d, k], facet=dest
+            )
+
+        for k in range(CHUNKS):
+            cut = slice(k * size, (k + 1) * size)
+            for d in range(1, half):
+                if k == 0:
+                    near[d].wait_recv()
+                send_buf[t, d, cut] = (part_o[d, cut] + near_buf[t, d, cut].astype(F32)).astype(BF16)
+                away(d, k).start()
         meanwhile()
         near[0].wait_recv()
-        total = part_o[0] + near_buf[t, 0].astype(F32)
-        for d in range(1, half):
-            far[d - 1].wait_recv()
-            total += far_buf[t, d].astype(F32)
-        adj[t, z] = total.astype(BF16)
-        size = rows // CHUNKS
-
         def hop(source, k, right):
             piece = adj.at[t, source, pl.ds(k * size, size)]
             sem = sr if right else sl
@@ -316,6 +314,12 @@
             return send(piece, piece, sem.at[t, source, k], rz.at[t, source, k], sub=to)
 
         for k in range(CHUNKS):
+            cut = slice(k * size, (k + 1) * size)
+            total = part_o[0, cut] + near_buf[t, 0, cut].astype(F32)
+            for d in range(1, half):
+                away(d, k).wait_recv()
+                total += far_buf[t, d, cut].astype(F32)
+            adj[t, z, cut] = total.astype(BF16)
 
             @pl.when(z < ns - 1)
             def _():
@@ -353,8 +357,11 @@
             def _():
                 use_column(z + d)
 
-        for copy in list(near.values()) + far:
+        for copy in near.values():
             copy.wait_send()
+        for d in range(1, half):
+            for k in range(CHUNKS):
+                away(d, k).wait_send()
         for d in range(0, ns):
             for k in range(CHUNKS):
 
@@ -394,14 +401,21 @@
 
         lax.fori_loop(0, STEP // lanes, chunk, 0)
 
-    gather_sections(0, subgrid_tables)
+    def first_tables():
+        subgrid_tables()
+        for d in range(ns - 1):
+            source = lax.rem(z - d - 1 + ns, ns)
+            send(o_ref, offs.at[source], s3.at[d], r3.at[d], sub=columns[d]).wait_recv()
+        lag_tables(0, ns // 2)
+
+    gather_sections(0, first_tables)
     sweep(False)
-    exchange(0, lag_tables, add_to_section)
+    exchange(0, lambda: lag_tables(ns // 2, ns), add_to_section)
     st[1, :SGW, :] = s_ref[:, :SGW].T.astype(BF16)
     st[1, SGW:, :] = s_ref[:, SGW:].T.astype(BF16)
-    gather_sections(1, image_tables)
+    gather_sections(1, lambda: image_tables(0, ns // 2))
     sweep(True)
-    exchange(1, lambda: None, add_to_image)
+    exchange(1, lambda: image_tables(ns // 2, ns), add_to_image)
 
 
 def local(model_image, step_sizes, facet_offsets, col_offsets, row_offsets, counts, vis_uv, vis_obs, vis_weight):
@@ -415,15 +429,8 @@
     dma = pltpu.SemaphoreType.DMA
     vmem = pl.BlockSpec(memory_space=VMEM)
     smem = pl.BlockSpec(memory_space=pltpu.SMEM)
-    image, residual = pl.pallas_call(
-        functools.partial(step_kernel, n, ns),
-        out_shape=(
-            jax.ShapeDtypeStruct(model.shape, F32),
-            jax.ShapeDtypeStruct((2, 1, 1, slots), F32),
-        ),
-        in_specs=[smem] * 5 + [pl.BlockSpec(memory_space=pl.ANY)] + [vmem] * 3,
-        out_specs=(vmem, vmem),
-        scratch_shapes=[
+    observed = jnp.transpose(vis_obs, (1, 2, 0, 3))
+    buffers = [
             VMEM((blocks * rows, STEP), BF16),
             VMEM((STEP, 2 * SGW), BF16),
             VMEM((rows, 2 * SGW), F32),
@@ -447,6 +454,18 @@
             VMEM((ns, blocks, 2 * SGW), F32),
             VMEM((ns, 2 * SGW, STEP), BF16),
             VMEM((blocks * rows, 2 * SGW), BF16),
+    ]
+    kept = 4 * (rows * width + 2 * slots) + 2**17
+    image, residual = pl.pallas_call(
+        functools.partial(step_kernel, n, ns),
+        out_shape=(
+            VMEM(model.shape, F32),
+            VMEM((2, 1, 1, slots), F32),
+        ),
+        in_specs=[smem] * 5 + [pl.BlockSpec(memory_space=pl.ANY)] + [vmem] * 3,
+        out_specs=(vmem, vmem),
+        scratch_shapes=buffers
+        + [
             dma((blocks,)),
             dma((ITERS, half)),
             dma((ITERS, half)),
@@ -456,15 +475,17 @@
             dma((ns,)),
             dma((ITERS, half)),
             dma((ITERS, half)),
-            dma((ITERS, half)),
-            dma((ITERS, half)),
+            dma((ITERS, half, CHUNKS)),
+            dma((ITERS, half, CHUNKS)),
             dma((ITERS, ns, CHUNKS)),
             dma((ITERS, ns, CHUNKS)),
             dma((ITERS, ns, CHUNKS)),
         ],
-        compiler_params=pltpu.CompilerParams(collective_id=0, has_side_effects=True),
+        compiler_params=pltpu.CompilerParams(
+            collective_id=0, has_side_effects=True, vmem_limit_bytes=VMEM_BYTES - kept
+        ),
         name="cycles",
-    )(step_sizes, facet_offsets, col_offsets, row_offsets, counts, model, vis_uv, vis_obs, vis_weight)
+    )(step_sizes, facet_offsets, col_offsets, row_offsets, counts, model, vis_uv, observed, vis_weight)
     return (image[None], residual)
 
 

time: 93.9 us -> 82.7 us (0.88)
  Pallas kernels: 85.7 us -> 78.5 us
  local copies, waits for them, and re-layouts: 6.59 us -> 2.63 us
    pallas_call x1, Pallas kernels: 85.7 us -> 78.5 us  [local(): pl.pallas_call(functools.partial(step_kernel, n, ns), out_shape=(VMEM(mod...]
    unnamed x5 -> x2, local copies, waits for them, and re-layouts: 6.59 us -> 2.63 us
where the time goes in v3:
time: 82.7 us; the launch traced here: 82.4 us
  Pallas kernels  78.5 us (95%)
  local copies, waits for them, and re-layouts  2.63 us (3%)
  between operations  1.29 us (2%)
    pallas_call x1, Pallas kernels, local(): pl.pallas_call(functools.partial(step_kernel, n, ns), out_shape=(VMEM(mod...  78.5 us
    unnamed x2, local copies, waits for them, and re-layouts  2.63 us

profile of v3, /device:TPU:0, one launch (start us, length us, event | category | flops | bytes accessed | tf_op | source)
XLA Modules:
  0.0 82.4 jit_solution(10278646451409897966)
XLA Ops:
  1.3 78.5 %cycles.1 = (f32[128,8192]{1,0:T(8,128)S(1)}, f32[2,1,1,4096]{3,2,1,0:T(1,128)S(1)}) custom-call(f32[2]{0:T(128)} %steps_ref.1, s32[2,8]{1,0:T(2,128)} %facet_ref.1, s32[1]{0:T(128)S(6)} %copy.15.col_ref, s32[1,8]{1,0:T(1,128)} %row_ref.1, s32[1,8]{1,0:T(1,128)} %count_ref.1, f32[128,8192]{1,0:T(8,128)} %bitcast.4, s32[2,1,1,4096]{3,2,1,0:T(1,128)} %pos_ref.1, ...), custom_call_target="tpu_custom_call" | custom-call | tf_op jit(solution)/shard_map/cycles/pallas_call | solution.py:459
  79.8 2.0 %copy.13 = f32[1,128,8192]{2,1,0:T(8,128)} copy(f32[1,128,8192]{2,1,0:T(8,128)S(1)} %bitcast.3) | data formatting | bytes 8388608
  81.8 0.6 copy.14
